TPU v7x, 128 devices: a 2x2x16 block of a 8x8x16 slice. The times are simulated.
128 devices in a mesh: member: 4 (over y, x), dp: 32 (over z, core).
Axes of the slice: x: 2, y: 2, z: 16, core: 2. Of those that a mesh axis runs over, the one named last changes fastest.
The devices are a block of a 8x8x16 slice.
Arguments:
- residual: bfloat16 [2048, 3072], P(('member', 'dp')), parts along dimension 0, may hold values from -6 to 6
- upstream: bfloat16 [2048, 3072], P(('member', 'dp')), parts along dimension 0, may hold values from -6 to 6
- gate_weight: bfloat16 [12288, 20480], P('member', 'dp'), parts along dimension 0, may hold values from -0.109375 to 0.109375
- up_weight: bfloat16 [12288, 20480], P('member', 'dp'), parts along dimension 0, may hold values from -0.109375 to 0.109375
- down_weight: bfloat16 [81920, 3072], P(('member', 'dp')), parts along dimension 0, may hold values from -0.0390625 to 0.0390625
- gain: float32 [12288], P('member'), parts along dimension 0, may hold values from 0.25 to 1.75
Outputs:
- grad_residual: bfloat16 [2048, 3072], P(('member', 'dp')), parts along dimension 0
- grad_gate: bfloat16 [12288, 20480], P('member', 'dp'), parts along dimension 0
- grad_up: bfloat16 [12288, 20480], P('member', 'dp'), parts along dimension 0
- grad_down: bfloat16 [81920, 3072], P(('member', 'dp')), parts along dimension 0
- grad_gain: float32 [12288], P('member'), parts along dimension 0
There are 4 independent parts, one for each index of `member`. A program takes and returns all parts, laid end to end along the dimension named above; each array names one. Nothing has to cross between parts.
All inputs are finite; a program needn't handle non-finite values.
Results may differ from a plain program's by a relative error of at most 0.0068.
Values may be sent and summed in bfloat16 or wider, within the bound.
A program may use at most 128 MiB of HBM per device.

v0:
```python
import jax
import jax.numpy as jnp
from jax import lax
from jax.sharding import Mesh
from jax.sharding import PartitionSpec as P

DP = ("dp_0", "dp_1")
MEMBER_DP = ("member", "dp_0", "dp_1")


norm_floor = 0.5
gelu_coeff = 0.7978845608
cubic_term = 0.044715


def reduced_to_own(tiles, axes, order):
    lengths = [lax.axis_size(a) for a in axes]
    tiles = tiles.reshape(*lengths, *tiles.shape[1:])
    tiles = tiles.transpose(*order, *range(len(axes), tiles.ndim))
    tiles = tiles.reshape(-1, *tiles.shape[len(axes) :])
    for k in order:
        tiles = lax.psum_scatter(tiles, axes[k], scatter_dimension=0, tiled=True)
    return tiles[0]


def in_blocks(shard, dim, size):
    before, after = (shard.shape[:dim], shard.shape[dim + 1 :])
    return jnp.moveaxis(shard.reshape(*before, size, -1, *after), dim, 0)


def summed_rows(shard, axes, order, dim):
    size = lax.axis_size(axes)
    return reduced_to_own(in_blocks(shard, dim, size), axes, order)


def copy_for_each(shard, axis):
    size = lax.axis_size(axis)
    return lax.all_to_all(
        jnp.broadcast_to(shard[None], (size, *shard.shape)), axis, 0, 0, tiled=True
    )


def taken_together(shard, axis):
    everything = copy_for_each(shard, axis)
    return jnp.sum(everything, axis=0)


def gelu_parts(gate_out):
    inner = jnp.tanh(gelu_coeff * (gate_out + cubic_term * gate_out * gate_out * gate_out))
    activated = 0.5 * gate_out * (1.0 + inner)
    gelu_slope = 0.5 * (1.0 + inner) + 0.5 * gate_out * (1.0 - inner * inner) * gelu_coeff * (
        1.0 + 3.0 * cubic_term * gate_out * gate_out
    )
    return (activated, gelu_slope)


def contract_last(left, right):
    return lax.dot_general(
        left, right, (((1,), (1,)), ((), ())), preferred_element_type=jnp.float32
    )


def contract_first(left, right):
    return lax.dot_general(
        left, right, (((0,), (0,)), ((), ())), preferred_element_type=jnp.float32
    )


def per_device(residual, upstream, gate_weight, up_weight, down_weight, gain):
    widened = residual.astype(jnp.float32)
    norm_scale = lax.rsqrt(jnp.mean(widened * widened, axis=1, keepdims=True) + norm_floor)
    unit_rows = widened * norm_scale
    normed = (unit_rows * gain).astype(jnp.bfloat16)
    normed_all = lax.all_gather(normed, DP, axis=0, tiled=True)
    gate_out = jnp.dot(normed_all, gate_weight, preferred_element_type=jnp.float32)
    up_out = jnp.dot(normed_all, up_weight, preferred_element_type=jnp.float32)
    activated, gelu_slope = gelu_parts(gate_out)
    hidden = (activated * up_out).astype(jnp.bfloat16)
    upstream_all = lax.all_gather(upstream, DP, axis=0, tiled=True)
    hidden_grad = contract_last(upstream_all, down_weight)
    grad_down = contract_first(hidden, upstream_all).astype(jnp.bfloat16)
    gate_grad = (hidden_grad * up_out * gelu_slope).astype(jnp.bfloat16)
    up_grad = (hidden_grad * activated).astype(jnp.bfloat16)
    grad_gate = contract_first(normed_all, gate_grad).astype(jnp.bfloat16)
    grad_up = contract_first(normed_all, up_grad).astype(jnp.bfloat16)
    partial_grad = contract_last(gate_grad, gate_weight) + contract_last(up_grad, up_weight)
    normed_grad = summed_rows(partial_grad, DP, (1, 0), 0)
    unit_grad = normed_grad * gain
    inner_mean = jnp.mean(unit_grad * unit_rows, axis=1, keepdims=True)
    grad_residual = (
        upstream.astype(jnp.float32) + norm_scale * (unit_grad - unit_rows * inner_mean)
    ).astype(jnp.bfloat16)
    grad_gain = taken_together(jnp.sum(normed_grad * unit_rows, axis=0), DP)
    return (grad_residual, grad_gate, grad_up, grad_down, grad_gain)


def solution(mesh):
    torus = Mesh(mesh.devices.reshape(mesh.shape["member"], 16, 2), ("member", "dp_0", "dp_1"))
    placed = (
        P(MEMBER_DP, None),
        P(MEMBER_DP, None),
        P("member", DP),
        P("member", DP),
        P(MEMBER_DP, None),
        P("member"),
    )
    return jax.shard_map(
        per_device,
        mesh=torus,
        in_specs=placed,
        out_specs=(
            P(MEMBER_DP, None),
            P("member", DP),
            P("member", DP),
            P(MEMBER_DP, None),
            P("member"),
        ),
        check_vma=False,
    )
```

profile of v0, /device:TPU:69, one launch (start us, length us, event | category | flops | bytes accessed | tf_op | source)
XLA Modules:
  0.0 312.8 jit_solution(6478909304152985722)
XLA Ops:
  7.2 0.1 all-gather.5.cloned.1.call-start
  7.2 1.0 fusion.18
  8.3 1.6 fusion.11
  9.9 0.1 all-gather.5.cloned.1.call-update
  10.0 0.1 all-gather.3.cloned.1.call-start
  10.1 0.7 all-gather.3.cloned.1.call-update
  10.8 0.1 reduce-scatter.3.cloned.1.call-start
  10.9 75.9 %all-gather.5.cloned.1.call-done = bf16[512,3072]{1,0:T(8,128)(2,1)} async-done(((bf16[16,3072]{1,0:T(8,128)(2,1)}), bf16[512,3072]{1,0:T(8,128)(2,1)}) %all-gather.5.cloned.1.call-update) | async-done | bytes 3145744 | tf_op jit(solution)/shard_map/all_gather | solution.py:74
  86.8 0.0 copy-start.6
  86.8 0.0 copy-start.8
  86.8 5.8 %fusion.23 = f32[512,640]{1,0:T(8,128)S(1)} fusion(bf16[512,3072]{1,0:T(8,128)(2,1)} %all-gather.5.cloned.1.call-done, bf16[3072,640]{1,0:T(8,128)(2,1)} %param.9), kind=kOutput, calls=%fused_computation.37 | convolution fusion | flops 2013265920 | bytes 8388608 | tf_op jit(solution)/shard_map/dot_general | solution.py:76
  92.6 0.0 copy-done.6
  92.6 0.0 copy-done.8
  92.6 2.6 fusion.24
  95.2 59.6 %all-gather.3.cloned.1.call-done = bf16[512,3072]{1,0:T(8,128)(2,1)} async-done(((bf16[16,3072]{1,0:T(8,128)(2,1)}), bf16[512,3072]{1,0:T(8,128)(2,1)}) %all-gather.3.cloned.1.call-update) | async-done | bytes 3145744 | tf_op jit(solution)/shard_map/all_gather | solution.py:79
  154.8 0.0 copy-start.7
  154.8 6.5 %multiply_convert_fusion.1 = (bf16[512,640]{1,0:T(8,128)(2,1)S(1)}, bf16[512,640]{1,0:T(8,128)(2,1)S(1)}) fusion(f32[512,640]{1,0:T(8,128)S(1)} %fusion.24, f32[512,640]{1,0:T(8,128)S(1)} %fusion.23, bf16[512,3072]{1,0:T(8,128)(2,1)} %all-gather.3.cloned.1.call-done, bf16[640,3072]{1,0:T(8,128)(2,1)} %param.10), kind=kOutput, calls=%fused_computation.14 | convolution fusion | flops 2020802560 | bytes 11010048 | tf_op jit(solution)/shard_map/dot_general | solution.py:58
  161.3 0.0 copy-start.9
  161.3 0.0 copy-done.7
  161.3 0.0 copy-start
  161.3 2.6 fusion.25
  164.0 0.0 copy-done.9
  164.0 0.0 copy-done
  164.0 2.7 convolution_add_fusion
  166.7 3.1 copy.13
  169.8 0.1 reduce-scatter.3.cloned.1.call-update
  169.9 0.2 reduce-scatter.5.cloned.1.call-start
  170.1 18.9 %reduce-scatter.3.cloned.1.call-done = f32[16,16,3072]{2,1,0:T(8,128)} async-done(((f32[32,16,3072]{2,1,0:T(8,128)}), f32[16,16,3072]{2,1,0:T(8,128)}) %reduce-scatter.3.cloned.1.call-update) | async-done | bytes 3145744 | tf_op jit(solution)/shard_map/reduce_scatter | solution.py:22
  189.0 0.1 reduce-scatter.5.cloned.1.call-update
  189.1 0.0 copy-start.2
  189.1 0.0 copy-start.5
  189.1 6.5 %convolution_convert_fusion.1 = bf16[3072,640]{1,0:T(8,128)(2,1)} fusion(bf16[512,3072]{1,0:T(8,128)(2,1)} %all-gather.5.cloned.1.call-done, bf16[512,640]{1,0:T(8,128)(2,1)S(1)} %get-tuple-element.7), kind=kOutput, calls=%fused_computation.1 | convolution fusion | flops 2015232000 | bytes 7733248 | tf_op jit(solution)/shard_map/dot_general | solution.py:64
  195.6 61.2 %reduce-scatter.5.cloned.1.call-done = f32[1,16,3072]{2,1,0:T(8,128)} async-done(((f32[16,16,3072]{2,1,0:T(8,128)}), f32[1,16,3072]{2,1,0:T(8,128)}) %reduce-scatter.5.cloned.1.call-update) | async-done | bytes 196624 | tf_op jit(solution)/shard_map/reduce_scatter | solution.py:22
  256.8 0.0 copy-done.2
  256.8 0.0 copy-done.5
  256.8 1.2 fusion.17
  257.9 0.9 broadcast_in_dim.2
  258.9 19.0 %all-to-all-start = ((f32[32,1,3072]{2,1,0:T(1,128)}), f32[32,1,3072]{2,1,0:T(1,128)S(1)}, u32[]{:S(2)}, u32[]{:S(2)}) async-start(f32[32,1,3072]{2,1,0:T(1,128)} %broadcast_in_dim.2), calls=%async_computation.2 | async-start | bytes 786432 | tf_op jit(solution)/shard_map/all_to_all | solution.py:38
  277.9 0.0 copy-start.1
  277.9 6.8 %convolution_convert_fusion.2 = bf16[3072,640]{1,0:T(8,128)(2,1)} fusion(bf16[512,3072]{1,0:T(8,128)(2,1)} %all-gather.5.cloned.1.call-done, bf16[512,640]{1,0:T(8,128)(2,1)} %copy-done.9), kind=kOutput, calls=%fused_computation.2 | convolution fusion | flops 2015232000 | bytes 7733248 | tf_op jit(solution)/shard_map/dot_general | solution.py:64
  284.6 0.0 copy-done.1
  284.7 0.0 copy-start.3
  284.7 0.0 copy-start.4
  284.7 4.3 %convolution_convert_fusion = bf16[640,3072]{1,0:T(8,128)(2,1)} fusion(bf16[512,3072]{1,0:T(8,128)(2,1)S(1)} %copy-done.1, f32[512,640]{1,0:T(8,128)S(1)} %fusion.23, f32[512,640]{1,0:T(8,128)S(1)} %fusion.24), kind=kOutput, calls=%fused_computation | convolution fusion | flops 2018508800 | bytes 9699328 | tf_op jit(solution)/shard_map/dot_general | solution.py:64
  289.0 0.0 copy-done.3
  289.0 0.0 copy-done.4
  289.0 0.8 fusion.16
  289.8 15.7 %all-to-all-done = f32[32,1,3072]{2,1,0:T(1,128)S(1)} async-done(((f32[32,1,3072]{2,1,0:T(1,128)}), f32[32,1,3072]{2,1,0:T(1,128)S(1)}, u32[]{:S(2)}, u32[]{:S(2)}) %all-to-all-start) | async-done | bytes 393248 | tf_op jit(solution)/shard_map/all_to_all | solution.py:38
  305.4 0.9 reduce_sum.39
  (2 shorter events, 0.0 us)
Async XLA Ops:
  7.2 79.6 %all-gather.5.cloned.1.call-start = ((), (), s32[]{:S(2)}) async-start(), calls=%async_computation.4 | async-start | bytes 3244032 | tf_op jit(solution)/shard_map/all_gather | solution.py:74
  10.0 144.8 %all-gather.3.cloned.1.call-start = ((), (), s32[]{:S(2)}) async-start(), calls=%async_computation.3 | async-start | bytes 3244032 | tf_op jit(solution)/shard_map/all_gather | solution.py:79
  10.8 178.2 %reduce-scatter.3.cloned.1.call-start = ((), (), s32[]{:S(2)}) async-start(), calls=%async_computation.5 | async-start | bytes 9437184 | tf_op jit(solution)/shard_map/reduce_scatter | solution.py:22
  86.8 5.8 %copy-start.6 = (bf16[3072,640]{1,0:T(8,128)(2,1)S(1)}, bf16[3072,640]{1,0:T(8,128)(2,1)}, u32[]{:S(2)}) copy-start(bf16[3072,640]{1,0:T(8,128)(2,1)} %param.8) | copy-start | bytes 11796484
  86.8 5.8 %copy-start.8 = (bf16[512,3072]{1,0:T(8,128)(2,1)S(1)}, bf16[512,3072]{1,0:T(8,128)(2,1)}, u32[]{:S(2)}) copy-start(bf16[512,3072]{1,0:T(8,128)(2,1)} %all-gather.5.cloned.1.call-done) | copy-start | bytes 9437188
  154.8 6.5 %copy-start.7 = (bf16[3072,640]{1,0:T(8,128)(2,1)S(1)}, bf16[3072,640]{1,0:T(8,128)(2,1)}, u32[]{:S(2)}) copy-start(bf16[3072,640]{1,0:T(8,128)(2,1)} %param.8) | copy-start | bytes 11796484
  161.3 2.7 copy-start.9
  161.3 2.7 copy-start
  169.9 86.9 %reduce-scatter.5.cloned.1.call-start = ((), (), s32[]{:S(2)}) async-start(), calls=%async_computation.6 | async-start | bytes 3342336 | tf_op jit(solution)/shard_map/reduce_scatter | solution.py:22
  189.1 67.7 %copy-start.2 = (bf16[16,3072]{1,0:T(8,128)(2,1)S(1)}, bf16[16,3072]{1,0:T(8,128)(2,1)}, u32[]{:S(2)}) copy-start(bf16[16,3072]{1,0:T(8,128)(2,1)} %param.6) | copy-start | bytes 294916
  189.1 67.7 %copy-start.5 = (f32[3072]{0:T(1024)S(1)}, f32[3072]{0:T(1024)}, u32[]{:S(2)}) copy-start(f32[3072]{0:T(1024)} %param.11) | copy-start | bytes 36868
  258.9 46.5 %all-to-all-start = ((f32[32,1,3072]{2,1,0:T(1,128)}), f32[32,1,3072]{2,1,0:T(1,128)S(1)}, u32[]{:S(2)}, u32[]{:S(2)}) async-start(f32[32,1,3072]{2,1,0:T(1,128)} %broadcast_in_dim.2), calls=%async_computation.2 | async-start | bytes 786432 | tf_op jit(solution)/shard_map/all_to_all | solution.py:38
  277.9 6.8 %copy-start.1 = (bf16[512,3072]{1,0:T(8,128)(2,1)S(1)}, bf16[512,3072]{1,0:T(8,128)(2,1)}, u32[]{:S(2)}) copy-start(bf16[512,3072]{1,0:T(8,128)(2,1)} %all-gather.3.cloned.1.call-done) | copy-start | bytes 9437188
  284.7 4.3 %copy-start.3 = (f32[1,16,3072]{2,1,0:T(8,128)S(1)}, f32[1,16,3072]{2,1,0:T(8,128)}, u32[]{:S(2)}) copy-start(f32[1,16,3072]{2,1,0:T(8,128)} %reduce-scatter.5.cloned.1.call-done) | copy-start | bytes 589828
  284.7 4.3 %copy-start.4 = (bf16[16,3072]{1,0:T(8,128)(2,1)S(1)}, bf16[16,3072]{1,0:T(8,128)(2,1)}, u32[]{:S(2)}) copy-start(bf16[16,3072]{1,0:T(8,128)(2,1)} %param.7) | copy-start | bytes 294916
Sparse Core Ops, SparseCore 0:
  10.3 76.4 all-gather.4
  88.5 66.2 all-gather.2
  170.0 18.9 reduce-scatter.2
  191.3 65.4 reduce-scatter.4
where the time goes:
time: 313 us
  waiting for transfers between devices  232 us (74%)
  matrix products  37.9 us (12%)
  starting transfers between devices  19.4 us (6%)
  between operations  13.9 us (4%)
  other arithmetic  5.46 us (2%)
  local copies, waits for them, and re-layouts  4.08 us (1%)
    reduce_scatter x2, waiting for transfers between devices, reduced_to_own(): tiles = lax.psum_scatter(tiles, axes[k], scatter_dimension=0, tiled=True)  80.1 us
    all_gather x1, waiting for transfers between devices, per_device(): normed_all = lax.all_gather(normed, DP, axis=0, tiled=True)  75.9 us
    all_gather x1, waiting for transfers between devices, per_device(): upstream_all = lax.all_gather(upstream, DP, axis=0, tiled=True)  59.6 us
    all_to_all x1, starting transfers between devices, copy_for_each(): lax.all_to_all(jnp.broadcast_to(shard[None], (size, *shard.shape)), axis,...  19 us
    dot_general x3, matrix products, contract_first(): lax.dot_general(left, right, (((0,), (0,)), ((), ())), preferred_element_...  17.6 us
    all_to_all x1, waiting for transfers between devices, copy_for_each(): lax.all_to_all(jnp.broadcast_to(shard[None], (size, *shard.shape)), axis,...  15.7 us
    dot_general x3, matrix products, contract_last(): lax.dot_general(left, right, (((1,), (1,)), ((), ())), preferred_element_...  11.8 us
  transfers between devices with their start and end apart: 5, of which 5 were waited for; matrix products, arithmetic and copies ran while one was open for 9% of the time, Pallas kernels for 0%

commit v1 on v0

v1 whole, which is shorter than its diff:
```python
import functools

import jax
import jax.numpy as jnp
from jax import lax
from jax.experimental import pallas as pl
from jax.experimental.pallas import tpu as pltpu
from jax.sharding import PartitionSpec as P

MESH = pl.DeviceIdType.MESH
F32 = jnp.float32
BF16 = jnp.bfloat16

norm_floor = 0.5
gelu_coeff = 0.7978845608
cubic_term = 0.044715

LANE = 128


def contract_last(left, right):
    return lax.dot_general(left, right, (((1,), (1,)), ((), ())), preferred_element_type=F32)


def contract_first(left, right):
    return lax.dot_general(left, right, (((0,), (0,)), ((), ())), preferred_element_type=F32)


def gelu_parts(gate_out):
    inner = jnp.tanh(gelu_coeff * (gate_out + cubic_term * gate_out * gate_out * gate_out))
    activated = 0.5 * gate_out * (1.0 + inner)
    gelu_slope = 0.5 * (1.0 + inner) + 0.5 * gate_out * (1.0 - inner * inner) * gelu_coeff * (
        1.0 + 3.0 * cubic_term * gate_out * gate_out
    )
    return activated, gelu_slope


def cut(total, most):
    size = most
    while total % size:
        size -= LANE
    return size


def kernel(
    chips, rows, width, units,
    res_ref, ups_ref, gw_ref, uw_ref, dw_ref, gain_ref,
    gres_ref, ggate_ref, gup_ref, gdown_ref, ggain_ref,
    tok, norm, scale, wgu, wd, act, slope, gu, hid,
    pown, pout, pin, sbuf, rbuf, gg, ggin, gring, ggend,
    wsem, own_sem, rs_send, rs_recv, ag_send, ag_recv, x_send, x_recv,
    p_send, p_recv, g_send, g_recv, gx_send, gx_recv,
):
    half = chips // 2
    group = chips // 2
    hw = width // 2
    grows = 2 * group * rows
    blocks = units // LANE

    me = lax.axis_index("dp")
    core = lax.rem(me, 2)
    chip = me // 2
    right = {"dp": lax.rem(chip + 1, chips) * 2 + core}
    left = {"dp": lax.rem(chip + chips - 1, chips) * 2 + core}
    partner = {"dp": me + 1 - 2 * core}
    ahead = (right, left)

    def hops(d, p):
        return half if d == p else half - 1

    def came(d, s):
        return chips - 1 if s == half else (2 * s - 1 if d == 0 else 2 * s)

    def goes(d, s):
        return chips - 1 if s == half else (2 * s if d == 0 else 2 * s - 1)

    def row0(slot, q):
        return (slot // group) * grows + q * group * rows + (slot % group) * rows

    def span(slot, q):
        return pl.ds(row0(slot, q), rows)

    def cols(p):
        return pl.ds(p * hw, hw)

    own = [
        pltpu.make_async_copy(src, tok.at[a, span(0, 0), :], own_sem.at[a])
        for a, src in enumerate((res_ref, ups_ref))
    ]
    for copy in own:
        copy.start()
    loads = []
    for b in range(blocks):
        for k, w in enumerate((gw_ref, uw_ref)):
            loads.append(
                pltpu.make_async_copy(
                    w.at[:, pl.ds(b * LANE, LANE)],
                    wgu.at[:, pl.ds((2 * b + k) * LANE, LANE)],
                    wsem.at[2 * b + k],
                )
            )
    loads.append(pltpu.make_async_copy(dw_ref, wd, wsem.at[2 * blocks]))
    for copy in loads:
        copy.start()

    barrier = pltpu.get_barrier_semaphore()
    for who in (left, right, partner):
        pl.semaphore_signal(barrier, inc=1, device_id=who, device_id_type=MESH)
    pl.semaphore_wait(barrier, 3)

    def ring_copy(a, d, p, s):
        src = 0 if s == 1 else came(d, s - 1)
        return pltpu.make_async_remote_copy(
            src_ref=tok.at[a, span(src, 0), cols(p)],
            dst_ref=tok.at[a, span(came(d, s), 0), cols(p)],
            send_sem=ag_send.at[a, d, p, s - 1],
            recv_sem=ag_recv.at[a, d, p, s - 1],
            device_id=ahead[d],
            device_id_type=MESH,
        )

    def side_copy(a, slot):
        return pltpu.make_async_remote_copy(
            src_ref=tok.at[a, span(slot, 0), :],
            dst_ref=tok.at[a, span(slot, 1), :],
            send_sem=x_send.at[a, slot],
            recv_sem=x_recv.at[a, slot],
            device_id=partner,
            device_id_type=MESH,
        )

    def prep(slot, q):
        at = span(slot, q)
        x = tok[0, at, :].astype(F32)
        sc = lax.rsqrt(jnp.mean(x * x, axis=1, keepdims=True) + norm_floor)
        scale[at, :] = jnp.broadcast_to(sc, (rows, LANE))
        norm[at, :] = ((x * sc) * gain_ref[...]).astype(BF16)

    def gate_up(g, b):
        at = pl.ds(g * grows, grows)
        both = jnp.dot(norm[at, :], wgu[:, pl.ds(2 * b * LANE, 2 * LANE)], preferred_element_type=F32)
        here = pl.ds(b * LANE, LANE)
        up_out = both[:, LANE:]
        activated, gelu_slope = gelu_parts(both[:, :LANE])
        act[:, here] = activated
        slope[:, here] = up_out * gelu_slope
        hid[at, here] = (activated * up_out).astype(BF16)

    def hidden_grad(g, b0, nb):
        at = pl.ds(g * grows, grows)
        hg = contract_last(tok[1, at, :], wd[pl.ds(b0 * LANE, nb * LANE), :])
        for k in range(nb):
            here = pl.ds((b0 + k) * LANE, LANE)
            piece = hg[:, k * LANE : (k + 1) * LANE]
            gu[at, pl.ds(2 * (b0 + k) * LANE, LANE)] = (piece * slope[:, here]).astype(BF16)
            gu[at, pl.ds((2 * (b0 + k) + 1) * LANE, LANE)] = (piece * act[:, here]).astype(BF16)

    pcut = cut(hw, 256)
    per_half = hw // pcut

    def partial(g, p, i):
        at = pl.ds(g * grows, grows)
        c0 = p * hw + i * pcut
        part = contract_last(gu[at, :], wgu[pl.ds(c0, pcut), :])
        unit = tok[0, at, pl.ds(c0, pcut)].astype(F32) * scale[at, 0:1]
        gain_part = jnp.sum(part * unit, axis=0, keepdims=True)
        here = pl.ds(i * pcut, pcut)
        if g == 0:
            gg[p, :, here] = gain_part
        else:
            gg[p, :, here] = gg[p, :, here] + gain_part
        pown[g, p, :, here] = part[: group * rows]
        pout[g, p, :, here] = part[group * rows :].astype(BF16)

    def share(g, p):
        return pltpu.make_async_remote_copy(
            src_ref=pout.at[g, p],
            dst_ref=pin.at[g, p],
            send_sem=p_send.at[g, p],
            recv_sem=p_recv.at[g, p],
            device_id=partner,
            device_id_type=MESH,
        )

    def group_work(g):
        late = []
        b0 = 0
        while b0 < blocks:
            nb = min(2, blocks - b0)
            late.append(functools.partial(hidden_grad, g, b0, nb))
            b0 += nb
        for p in range(2):
            for i in range(per_half):
                late.append(functools.partial(partial, g, p, i))
            late.append(lambda p=p: share(g, p).start())
        return [functools.partial(gate_up, g, b) for b in range(blocks)], late

    own[0].wait()
    for p in range(2):
        for d in range(2):
            ring_copy(0, d, p, 1).start()
    own[1].wait()
    for p in range(2):
        for d in range(2):
            ring_copy(1, d, p, 1).start()
    side_copy(0, 0).start()
    side_copy(1, 0).start()
    prep(0, 0)

    def arrivals(a, s, p):
        for d in range(2):
            if s <= hops(d, p):
                ring_copy(a, d, p, s).wait_recv()
                if s < hops(d, p):
                    ring_copy(a, d, p, s + 1).start()

    def slots_of(s):
        return [0] if s == 0 else ([chips - 1] if s == half else [came(0, s), came(1, s)])

    def sides(a, s):
        for slot in slots_of(s):
            side_copy(a, slot).start()

    waited = set()

    def side_waits(a, s):
        if (a, s) in waited:
            return
        waited.add((a, s))
        for slot in slots_of(s):
            side_copy(a, slot).wait_recv()
            if a == 0:
                prep(slot, 1)

    ready = half // 2

    def once_here(a, work):
        for s in range(ready + 1):
            side_waits(a, s)
        work()

    first_now, first_late = group_work(0)
    first = [functools.partial(once_here, 0, work) for work in first_now]
    first += [functools.partial(once_here, 1, work) for work in first_late]
    places = 4 * (half - ready - 1) + 2
    done = 0
    place = 0
    for s in range(1, half):
        for a in range(2):
            for p in range(2):
                arrivals(a, s, p)
                if p == 0:
                    side_waits(a, s - 1)
                if s > ready:
                    if place == 0:
                        for copy in loads:
                            copy.wait()
                    place += 1
                    upto = min(len(first), -(-len(first) * place // places))
                    for work in first[done:upto]:
                        work()
                    done = upto
            sides(a, s)
            if a == 0:
                for slot in slots_of(s):
                    prep(slot, 0)
    if place == 0:
        for copy in loads:
            copy.wait()
    for work in first[done:]:
        work()
    second_now, second_late = group_work(1)
    for p in range(2):
        arrivals(0, half, p)
    sides(0, half)
    prep(chips - 1, 0)
    side_waits(0, half - 1)
    side_waits(0, half)
    for work in second_now[:-1]:
        work()
    for p in range(2):
        arrivals(1, half, p)
    sides(1, half)
    second_now[-1]()
    side_waits(1, half - 1)
    side_waits(1, half)
    for work in second_late:
        work()

    gain_side = pltpu.make_async_remote_copy(
        src_ref=gg.at[1 - core], dst_ref=ggin, send_sem=gx_send.at[0], recv_sem=gx_recv.at[0],
        device_id=partner, device_id_type=MESH,
    )
    gain_side.start()

    def chain(d, p, i):
        return pltpu.make_async_remote_copy(
            src_ref=sbuf.at[d, p, i - 1], dst_ref=rbuf.at[d, p, i - 1],
            send_sem=rs_send.at[d, p, i - 1], recv_sem=rs_recv.at[d, p, i - 1],
            device_id=ahead[d], device_id_type=MESH,
        )

    def gain_hop(d, i):
        return pltpu.make_async_remote_copy(
            src_ref=gring.at[d, i - 1], dst_ref=gring.at[d, i],
            send_sem=g_send.at[d, i - 1], recv_sem=g_recv.at[d, i - 1],
            device_id=ahead[d], device_id_type=MESH,
        )

    def total(slot, p):
        g = slot // group
        at = pl.ds((slot % group) * rows, rows)
        return pown[g, p, at, :] + pin[g, p, at, :].astype(F32)

    def pass_on(d, p, i):
        count = hops(d, p)
        value = total(goes(d, count + 1 - i), p)
        if i > 1:
            value = value + rbuf[d, p, i - 2].astype(F32)
        sbuf[d, p, i - 1] = value.astype(BF16)
        chain(d, p, i).start()

    dcut = cut(width, 384)
    ucut = cut(width, 768)

    def grad_in(i):
        here = pl.ds(i * dcut, dcut)
        out = contract_first(norm[:, here], gu[...]).astype(BF16)
        for b in range(blocks):
            at = pl.ds(b * LANE, LANE)
            ggate_ref[here, at] = out[:, 2 * b * LANE : (2 * b + 1) * LANE]
            gup_ref[here, at] = out[:, (2 * b + 1) * LANE : (2 * b + 2) * LANE]

    def grad_out(i):
        here = pl.ds(i * ucut, ucut)
        gdown_ref[:, here] = contract_first(hid[...], tok[1, :, here]).astype(BF16)

    fill = [functools.partial(grad_in, i) for i in range(width // dcut)]
    fill += [functools.partial(grad_out, i) for i in range(width // ucut)]

    for g in (1, 0):
        for p in range(2):
            share(g, p).wait_recv()
    for d in range(2):
        for p in range(2):
            pass_on(d, p, 1)
    gain_side.wait_recv()
    for d in range(2):
        gring[d, 0] = gg[core] + ggin[...]
    gain_count = (half, half - 1)
    for d in range(2):
        gain_hop(d, 1).start()

    done = 0
    for i in range(1, half + 1):
        upto = len(fill) * i // half
        for work in fill[done:upto]:
            work()
        done = upto
        for d in range(2):
            for p in range(2):
                if i <= hops(d, p):
                    chain(d, p, i).wait_recv()
                    if i < hops(d, p):
                        pass_on(d, p, i + 1)
        for d in range(2):
            if i <= gain_count[d]:
                gain_hop(d, i).wait_recv()
                if i < gain_count[d]:
                    gain_hop(d, i + 1).start()

    gain_sum = gring[0, 0]
    for d in range(2):
        for i in range(1, gain_count[d] + 1):
            gain_sum = gain_sum + gring[d, i]
    ggend[core] = gain_sum
    gain_back = pltpu.make_async_remote_copy(
        src_ref=ggend.at[core], dst_ref=ggend.at[core], send_sem=gx_send.at[1], recv_sem=gx_recv.at[1],
        device_id=partner, device_id_type=MESH,
    )
    gain_back.start()

    at = span(0, 0)
    sc = scale[at, 0:1]
    unit_rows = tok[0, at, :].astype(F32) * sc
    unit_grad = []
    for p in range(2):
        value = total(0, p)
        for d in range(2):
            value = value + rbuf[d, p, hops(d, p) - 1].astype(F32)
        unit_grad.append(value * gain_ref[:, cols(p)])
    sums = 0.0
    for p in range(2):
        sums = sums + jnp.sum(unit_grad[p] * unit_rows[:, p * hw : (p + 1) * hw], axis=1, keepdims=True)
    inner_mean = sums / width
    for p in range(2):
        unit = unit_rows[:, p * hw : (p + 1) * hw]
        gres_ref[:, cols(p)] = (
            tok[1, at, cols(p)].astype(F32) + sc * (unit_grad[p] - unit * inner_mean)
        ).astype(BF16)

    for a in range(2):
        for d in range(2):
            for p in range(2):
                for s in range(1, hops(d, p) + 1):
                    ring_copy(a, d, p, s).wait_send()
        for slot in range(chips):
            side_copy(a, slot).wait_send()
    for g in range(2):
        for p in range(2):
            share(g, p).wait_send()
    for d in range(2):
        for p in range(2):
            for i in range(1, hops(d, p) + 1):
                chain(d, p, i).wait_send()
        for i in range(1, gain_count[d] + 1):
            gain_hop(d, i).wait_send()
    gain_side.wait_send()
    gain_back.wait()
    ggain_ref[...] = ggend[...]


def per_device(chips, residual, upstream, gate_weight, up_weight, down_weight, gain):
    rows, width = residual.shape
    units = gate_weight.shape[1]
    half = chips // 2
    hw = width // 2
    group = chips // 2
    all_rows = 2 * chips * rows
    vmem = pl.BlockSpec(memory_space=pltpu.VMEM)
    anywhere = pl.BlockSpec(memory_space=pl.ANY)
    dma = pltpu.SemaphoreType.DMA
    outs = pl.pallas_call(
        functools.partial(kernel, chips, rows, width, units),
        out_shape=(
            jax.ShapeDtypeStruct((rows, width), BF16),
            jax.ShapeDtypeStruct((width, units), BF16),
            jax.ShapeDtypeStruct((width, units), BF16),
            jax.ShapeDtypeStruct((units, width), BF16),
            jax.ShapeDtypeStruct((2, 1, hw), F32),
        ),
        in_specs=[anywhere] * 5 + [vmem],
        out_specs=(vmem,) * 5,
        scratch_shapes=[
            pltpu.VMEM((2, all_rows, width), BF16),
            pltpu.VMEM((all_rows, width), BF16),
            pltpu.VMEM((all_rows, LANE), F32),
            pltpu.VMEM((width, 2 * units), BF16),
            pltpu.VMEM((units, width), BF16),
            pltpu.VMEM((all_rows // 2, units), F32),
            pltpu.VMEM((all_rows // 2, units), F32),
            pltpu.VMEM((all_rows, 2 * units), BF16),
            pltpu.VMEM((all_rows, units), BF16),
            pltpu.VMEM((2, 2, group * rows, hw), F32),
            pltpu.VMEM((2, 2, group * rows, hw), BF16),
            pltpu.VMEM((2, 2, group * rows, hw), BF16),
            pltpu.VMEM((2, 2, half, rows, hw), BF16),
            pltpu.VMEM((2, 2, half, rows, hw), BF16),
            pltpu.VMEM((2, 1, hw), F32),
            pltpu.VMEM((1, hw), F32),
            pltpu.VMEM((2, half + 1, 1, hw), F32),
            pltpu.VMEM((2, 1, hw), F32),
            dma((2 * units // LANE + 1,)),
            dma((2,)),
            dma((2, 2, half)),
            dma((2, 2, half)),
            dma((2, 2, 2, half)),
            dma((2, 2, 2, half)),
            dma((2, chips)),
            dma((2, chips)),
            dma((2, 2)),
            dma((2, 2)),
            dma((2, half)),
            dma((2, half)),
            dma((2,)),
            dma((2,)),
        ],
        compiler_params=pltpu.CompilerParams(
            collective_id=0, has_side_effects=True, vmem_limit_bytes=VMEM_LIMIT
        ),
        name="ffn_backward",
    )(residual, upstream, gate_weight, up_weight, down_weight, gain.reshape(1, width))
    grad_residual, grad_gate, grad_up, grad_down, grad_gain = outs
    return grad_residual, grad_gate, grad_up, grad_down, grad_gain.reshape(width)


VMEM_LIMIT = 40 * 1024 * 1024


def solution(mesh):
    both = P(("member", "dp"), None)
    split = P("member", "dp")
    return jax.shard_map(
        functools.partial(per_device, mesh.shape["dp"] // 2),
        mesh=mesh,
        in_specs=(both, both, split, split, both, P("member")),
        out_specs=(both, split, split, both, P("member")),
        check_vma=False,
    )
```

time: 313 us -> 104 us (0.33)
  waiting for transfers between devices: 232 us -> 0 us
  Pallas kernels: 0 us -> 94 us
  matrix products: 37.9 us -> 0 us
  starting transfers between devices: 19.4 us -> 0 us
  between operations: 13.9 us -> 0.65 us
  other arithmetic: 5.46 us -> 0 us
  local copies, waits for them, and re-layouts: 4.08 us -> 9.49 us
    all_gather x2 -> x0, waiting for transfers between devices: 136 us -> none  [the longest x1 75.9 us: per_device(): normed_all = lax.all_gather(normed, DP, axis=0, tiled=True)]
    pallas_call x0 -> x1, Pallas kernels: none -> 94 us  [per_device(): pl.pallas_call(functools.partial(kernel, chips, rows, width, units), out_...]
    reduce_scatter x2 -> x0, waiting for transfers between devices: 80.1 us -> none  [reduced_to_own(): tiles = lax.psum_scatter(tiles, axes[k], scatter_dimension=0, tiled=True)]
    dot_general x8 -> x0, matrix products: 37.9 us -> none  [the longest x3 17.6 us: contract_first(): lax.dot_general(left, right, (((0,), (0,)), ((), ())), preferred_element_...]
    all_to_all x1 -> x0, starting transfers between devices: 19 us -> none  [copy_for_each(): lax.all_to_all(jnp.broadcast_to(shard[None], (size, *shard.shape)), axis,...]
    all_to_all x1 -> x0, waiting for transfers between devices: 15.7 us -> none  [copy_for_each(): lax.all_to_all(jnp.broadcast_to(shard[None], (size, *shard.shape)), axis,...]
    unnamed x20 -> x11, local copies, waits for them, and re-layouts: 0.05 us -> 9.49 us
  transfers between devices with their start and end apart: 5 -> 0, of which waited for: 5 -> 0; matrix products, arithmetic and copies ran while one was open for 9% -> 0% of each run, Pallas kernels for 0% -> 0%
where the time goes in v1:
time: 104 us
  Pallas kernels  94 us (90%)
  local copies, waits for them, and re-layouts  9.49 us (9%)
    pallas_call x1, Pallas kernels, per_device(): pl.pallas_call(functools.partial(kernel, chips, rows, width, units), out_...  94 us
    unnamed x11, local copies, waits for them, and re-layouts  9.49 us

profile of v1, /device:TPU:69, one launch (start us, length us, event | category | flops | bytes accessed | tf_op | source)
XLA Modules:
  0.0 104.1 jit_solution(10060887700355142238)
XLA Ops:
  0.6 0.0 copy-start
  0.6 0.9 copy-done
  1.5 0.0 copy-start.1
  1.5 0.9 copy-done.1
  2.4 0.0 copy-start.2
  2.4 0.7 copy-done.2
  3.1 94.0 %ffn_backward.1 = (bf16[16,3072]{1,0:T(8,128)(2,1)S(1)}, bf16[3072,640]{1,0:T(8,128)(2,1)S(1)}, bf16[3072,640]{1,0:T(8,128)(2,1)S(1)}, bf16[640,3072]{1,0:T(8,128)(2,1)S(1)}, f32[2,1,1536]{2,1,0:T(1,128)S(1)}) custom-call(bf16[16,3072]{1,0:T(8,128)(2,1)S(1)} %copy-done, bf16[16,3072]{1,0:T(8,128)(2,1)S(1)} %copy-done.1, bf16[3072,640]{1,0:T(8,128)(2,1)} %gw_ref.1, ...), custom_call_target="tpu_custom_call" | custom-call | tf_op jit(solution)/shard_map/ffn_backward/pallas_call | solution.py:433
  97.1 0.6 copy.16
  97.7 1.9 %copy.17 = bf16[3072,640]{1,0:T(8,128)(2,1)} copy(bf16[3072,640]{1,0:T(8,128)(2,1)S(1)} %get-tuple-element.21) | data formatting | bytes 7864320
  99.7 1.9 %copy.18 = bf16[3072,640]{1,0:T(8,128)(2,1)} copy(bf16[3072,640]{1,0:T(8,128)(2,1)S(1)} %get-tuple-element.22) | data formatting | bytes 7864320
  101.6 1.9 %copy.19 = bf16[640,3072]{1,0:T(8,128)(2,1)} copy(bf16[640,3072]{1,0:T(8,128)(2,1)S(1)} %get-tuple-element.23) | data formatting | bytes 7864320
  103.5 0.6 copy.20
Async XLA Ops:
  0.6 0.9 copy-start
  1.5 0.9 copy-start.1
  2.4 0.7 copy-start.2
